TPU v7x, 32 devices: a 4x4x1 block of a 4x4x8 slice. The times are simulated.
32 devices in a mesh: pod: 1 (over z), data: 4 (over y), col: 4 (over x), row: 2 (over core).
Axes of the slice: x: 4, y: 4, z: 1, core: 2. Of those that a mesh axis runs over, the one named last changes fastest.
The devices are a block of a 4x4x8 slice.
Arguments:
- x_act: bfloat16 [8192, 2048], P(('pod', 'data', 'row'), 'col')
- w_fused: bfloat16 [2048, 22016], P(('pod', 'row'), 'col')
- dy_out: bfloat16 [8192, 22016], P(('pod', 'data', 'row'), 'col')
Outputs:
- output 1: bfloat16 [8192, 2048], P(('pod', 'data', 'row'), 'col')
- output 2: float32 [2048, 22016], P(('pod', 'data', 'row'), 'col')
All inputs are finite; a program needn't handle non-finite values.
Results may differ from a plain program's by a relative error of at most 0.001.
Values are sent between devices in bfloat16 or wider.
A program may use at most 768 MiB of HBM per device.

v0:
```python
import jax
import jax.numpy as jnp
from jax import lax
from jax.sharding import PartitionSpec as P


def solution(mesh):
    act_spec = P(("pod", "data", "row"), "col")
    wgt_spec = P(("pod", "row"), "col")

    def local_step(x_blk, w_blk, dy_blk):
        w_cols = lax.all_gather(w_blk, "row", axis=0, tiled=True)
        dx_part = lax.dot_general(dy_blk, w_cols, (((1,), (1,)), ((), ())), preferred_element_type=jnp.float32)
        dx_blk = lax.psum_scatter(dx_part, "col", scatter_dimension=1, tiled=True).astype(jnp.bfloat16)
        x_rows = lax.all_gather(x_blk, "col", axis=1, tiled=True)
        dw_part = lax.dot_general(x_rows, dy_blk, (((0,), (0,)), ((), ())), preferred_element_type=jnp.float32)
        dw_blk = lax.psum_scatter(dw_part, ("data", "row"), scatter_dimension=0, tiled=True)
        return dx_blk, dw_blk

    return jax.shard_map(local_step, mesh=mesh, in_specs=(act_spec, wgt_spec, act_spec), out_specs=(act_spec, act_spec), check_vma=False)
```

profile of v0, /device:TPU:97, one launch (start us, length us, event | category | flops | bytes accessed | tf_op | source)
XLA Modules:
  0.0 411.5 jit_solution(13775932996952359094)
XLA Ops:
  7.2 0.1 all-gather.3.cloned.1.call-start
  7.2 0.7 all-gather.3.cloned.1.call-update
  8.0 0.1 all-gather.5.cloned.1.call-start
  8.0 0.7 all-gather.5.cloned.1.call-update
  8.8 0.1 reduce-scatter.3.cloned.1.call-start
  8.8 42.8 %all-gather.3.cloned.1.call-done = bf16[2048,5504]{1,0:T(8,128)(2,1)} async-done(((bf16[1024,5504]{1,0:T(8,128)(2,1)}), bf16[2048,5504]{1,0:T(8,128)(2,1)}) %all-gather.3.cloned.1.call-update) | async-done | bytes 22544400 | tf_op jit(solution)/shard_map/all_gather | solution.py:12
  51.6 31.8 %fusion = f32[1024,2048]{1,0:T(8,128)} fusion(bf16[1024,5504]{1,0:T(8,128)(2,1)} %param.5, bf16[2048,5504]{1,0:T(8,128)(2,1)} %all-gather.3.cloned.1.call-done), kind=kOutput, calls=%fused_computation | convolution fusion | flops 23085449216 | bytes 42205184 | tf_op jit(solution)/shard_map/dot_general | solution.py:13
  83.4 0.1 reduce-scatter.3.cloned.1.call-update
  83.5 0.1 reduce-scatter.5.cloned.1.call-start
  83.5 16.0 %all-gather.5.cloned.1.call-done = bf16[1024,2048]{1,0:T(8,128)(2,1)} async-done(((bf16[1024,512]{1,0:T(8,128)(2,1)}), bf16[1024,2048]{1,0:T(8,128)(2,1)}) %all-gather.5.cloned.1.call-update) | async-done | bytes 4194320 | tf_op jit(solution)/shard_map/all_gather | solution.py:15
  99.6 33.6 %fusion.1 = f32[2048,5504]{1,0:T(8,128)} fusion(bf16[1024,2048]{1,0:T(8,128)(2,1)} %all-gather.5.cloned.1.call-done, bf16[1024,5504]{1,0:T(8,128)(2,1)} %param.5), kind=kOutput, calls=%fused_computation.1 | convolution fusion | flops 23085449216 | bytes 60555264 | tf_op jit(solution)/shard_map/dot_general | solution.py:16
  133.1 0.1 reduce-scatter.5.cloned.1.call-update
  133.2 47.2 %reduce-scatter.3.cloned.1.call-done = f32[1024,512]{1,0:T(8,128)} async-done(((f32[1024,2048]{1,0:T(8,128)}), f32[1024,512]{1,0:T(8,128)}) %reduce-scatter.3.cloned.1.call-update) | async-done | bytes 2097168 | tf_op jit(solution)/shard_map/reduce_scatter | solution.py:14
  180.4 2.7 convert_element_type.3
  183.1 221.9 %reduce-scatter.5.cloned.1.call-done = f32[256,5504]{1,0:T(8,128)} async-done(((f32[2048,5504]{1,0:T(8,128)}), f32[256,5504]{1,0:T(8,128)}) %reduce-scatter.5.cloned.1.call-update) | async-done | bytes 5636112 | tf_op jit(solution)/shard_map/reduce_scatter | solution.py:17
Async XLA Ops:
  7.2 44.4 %all-gather.3.cloned.1.call-start = ((), (), s32[]{:S(2)}) async-start(), calls=%async_computation.2 | async-start | bytes 33816576 | tf_op jit(solution)/shard_map/all_gather | solution.py:12
  8.0 91.6 %all-gather.5.cloned.1.call-start = ((), (), s32[]{:S(2)}) async-start(), calls=%async_computation.4 | async-start | bytes 5242880 | tf_op jit(solution)/shard_map/all_gather | solution.py:15
  8.8 171.6 %reduce-scatter.3.cloned.1.call-start = ((), (), s32[]{:S(2)}) async-start(), calls=%async_computation.3 | async-start | bytes 10485760 | tf_op jit(solution)/shard_map/reduce_scatter | solution.py:14
  83.5 321.5 %reduce-scatter.5.cloned.1.call-start = ((), (), s32[]{:S(2)}) async-start(), calls=%async_computation.5 | async-start | bytes 50724864 | tf_op jit(solution)/shard_map/reduce_scatter | solution.py:17
Sparse Core Ops, SparseCore 0:
  9.6 41.9 all-gather.2
  53.2 46.3 all-gather.4
  101.9 78.3 reduce-scatter.2
  183.2 221.7 reduce-scatter.4
where the time goes:
time: 412 us; the launch traced here: 411 us
  waiting for transfers between devices  329 us (80%)
  matrix products  65.4 us (16%)
  between operations  13.8 us (3%)
    reduce_scatter x1, waiting for transfers between devices, local_step(): lax.psum_scatter(dw_part, ('data', 'row'), scatter_dimension=0, tiled=True)  222 us
    reduce_scatter x1, waiting for transfers between devices, local_step(): lax.psum_scatter(dx_part, 'col', scatter_dimension=1, tiled=True)  47.2 us
    all_gather x1, waiting for transfers between devices, local_step(): w_cols = lax.all_gather(w_blk, 'row', axis=0, tiled=True)  42.8 us
    dot_general x1, matrix products, local_step(): lax.dot_general(x_rows, dy_blk, (((0,), (0,)), ((), ())), preferred_eleme...  33.6 us
    dot_general x1, matrix products, local_step(): lax.dot_general(dy_blk, w_cols, (((1,), (1,)), ((), ())), preferred_eleme...  31.8 us
    all_gather x1, waiting for transfers between devices, local_step(): x_rows = lax.all_gather(x_blk, 'col', axis=1, tiled=True)  16 us
  transfers between devices with their start and end apart: 4, of which 4 were waited for; matrix products, arithmetic and copies ran while one was open for 17% of the time, Pallas kernels for 0%

commit v1 on v0

v1 whole, which is shorter than its diff:
```python
import functools

import jax
import jax.numpy as jnp
from jax import lax
from jax.experimental import pallas as pl
from jax.experimental.pallas import tpu as pltpu
from jax.sharding import PartitionSpec as P

MESH = pl.DeviceIdType.MESH
F32, BF16 = jnp.float32, jnp.bfloat16

ARRIVAL = ((0, 0), (0, 1), (1, 0), (3, 1), (1, 1), (3, 0), (2, 0), (2, 1))
WIDE = 1024
TILE = 256
DEPTH = 512


def kernel(nd, nc, x_ref, w_ref, dy_ref, dx_ref, dw_ref, dyo, wo, tail_y,
           xg, xt, part, relay_y, acc, relay_x, tail_x, buf, stage,
           sem_g, rem_g, sem_gp, sem_gf, loc_x, sem_a, rem_a, sem_w, rem_w, loc_d,
           sem_y, rem_y, sem_x, rem_x, loc_s, loc_o, loc_w, loc_dx):
    d, c, r = lax.axis_index("data"), lax.axis_index("col"), lax.axis_index("row")
    tokens, cols = dy_ref.shape
    half = xg.shape[3]
    band = 2 * half
    d_up, d_dn = (d + 1) % nd, (d + nd - 1) % nd
    c_up, c_dn = (c + 1) % nc, (c + nc - 1) % nc
    other = 1 - r
    mine = pl.ds(pl.multiple_of(r * tokens, tokens), tokens)
    theirs = pl.ds(pl.multiple_of(other * tokens, tokens), tokens)
    chunks = [(lo, min(WIDE, cols - lo)) for lo in range(0, cols, WIDE)]

    def rcopy(src, dst, send, recv, **to):
        return pltpu.make_async_remote_copy(src_ref=src, dst_ref=dst, send_sem=send, recv_sem=recv,
                                            device_id=to, device_id_type=MESH)

    def lcopy(src, dst, sem):
        return pltpu.make_async_copy(src, dst, sem)

    def x_local(t):
        return lcopy(x_ref.at[:, pl.ds(pl.multiple_of(r * band + t * half, half), half)], xg.at[0, t, mine], loc_x.at[t])

    def x_partner(t):
        return rcopy(x_ref.at[:, pl.ds(pl.multiple_of(other * band + t * half, half), half)], xg.at[0, t, mine],
                     sem_gp.at[t], rem_g.at[0, t, r], row=other)

    def x_send(up, core, t):
        slot = 3 if up else 1
        return rcopy(x_ref.at[:, pl.ds(core * band + t * half, half)], xg.at[slot, t, mine],
                     sem_g.at[up, core, t], rem_g.at[slot, t, r], col=c_up if up else c_dn, row=core)

    def x_pass(up, t):
        src, rows, who = (3, pl.ds(0, tokens), 0) if up else (1, pl.ds(tokens, tokens), 1)
        return rcopy(xg.at[src, t, rows], xg.at[2, t, rows], sem_gf.at[up, t], rem_g.at[2, t, who],
                     col=c_up if up else c_dn)

    def x_arrived(k, t, who):
        rows = pl.ds(pl.multiple_of(who * tokens, tokens), tokens)
        return rcopy(xg.at[k, t, rows], xg.at[k, t, rows], sem_gp.at[0], rem_g.at[k, t, who], row=other)

    def dy_swap(j):
        lo, w = chunks[j]
        dst = buf.at[j, mine, pl.ds(0, w)] if j < 2 else dyo.at[:, pl.ds(lo, w)]
        return rcopy(dy_ref.at[:, pl.ds(lo, w)], dst, sem_a.at[j], rem_a.at[j], row=other)

    def dy_arrived(j):
        lo, w = chunks[j]
        dst = buf.at[j, theirs, pl.ds(0, w)] if j < 2 else dyo.at[:, pl.ds(lo, w)]
        return rcopy(dy_ref.at[:, pl.ds(lo, w)], dst, sem_a.at[j], rem_a.at[j], row=other)

    def dy_load(j):
        lo, w = chunks[j]
        return lcopy(dy_ref.at[:, pl.ds(lo, w)], buf.at[j % 2, mine, pl.ds(0, w)], loc_d.at[j % 2, 0])

    def dyo_load(j):
        lo, w = chunks[j]
        return lcopy(dyo.at[:, pl.ds(lo, w)], buf.at[j % 2, theirs, pl.ds(0, w)], loc_d.at[j % 2, 1])

    def w_swap():
        return rcopy(w_ref, wo, sem_w, rem_w, row=other)

    def y_msg(m, j):
        at = pl.ds(*chunks[j])
        k, t = ((2, 1), (2, 0), (1, 0), (3, 1), (1, 1), (3, 0))[m]
        down = m % 2
        dst = relay_y.at[down, :, at] if m < 2 else tail_y.at[t, down, :, at]
        return rcopy(part.at[k, t, :, at], dst, sem_y.at[m, j], rem_y.at[m, j], data=d_dn if down else d_up)

    def x_msg(m):
        k, t = ((2, 1), (2, 0), (1, 0), (3, 1), (1, 1), (3, 0))[m]
        down = m % 2
        dst = relay_x.at[down] if m < 2 else tail_x.at[t, down]
        return rcopy(acc.at[k, t], dst, sem_x.at[m], rem_x.at[m], col=c_dn if down else c_up)

    for t in range(2):
        x_local(t).start()
    for j in range(2):
        dy_load(j).start()

    barrier = pltpu.get_barrier_semaphore()
    peers = [dict(row=other), dict(data=d_up), dict(data=d_dn)]
    peers += [dict(col=n, row=k) for n in (c_up, c_dn) for k in range(2)]
    for peer in peers:
        pl.semaphore_signal(barrier, inc=1, device_id=peer, device_id_type=MESH)
    pl.semaphore_wait(barrier, len(peers))

    for t in range(2):
        x_partner(t).start()
    dy_swap(0).start()
    for turn in range(2):
        for core in range(2):
            x_send(1, core, 1 - turn).start()
            x_send(0, core, turn).start()
    for j in range(1, len(chunks)):
        dy_swap(j).start()
    w_swap().start()

    def turn_block(i):
        k, t = ARRIVAL[i]

        def step(b, _):
            rows = pl.ds(pl.multiple_of(b * 512, 512), 512)
            xt[i, :, rows] = xg[k, t, rows, :].T
            return 0

        lax.fori_loop(0, 2 * tokens // 512, step, 0)

    def product(first, count, j):
        lo, w = chunks[j]

        def one(at, width):
            lhs = xt[first:first + count].reshape(count * half, 2 * tokens)
            rhs = buf[j % 2, :, pl.ds(at, width)]
            out = lax.dot_general(lhs, rhs, (((1,), (0,)), ((), ())), preferred_element_type=F32)
            for n in range(count):
                k, t = ARRIVAL[first + n]
                part[(k + c - d + nd) % nd, t, :, pl.ds(pl.multiple_of(lo + at, 128), width)] = out[n * half:(n + 1) * half]

        def step(b, _):
            one(pl.multiple_of(b * TILE, TILE), TILE)
            return 0

        lax.fori_loop(0, w // TILE, step, 0)
        if w % TILE:
            one(w - w % TILE, w % TILE)

    early = min(2, len(chunks))
    for s in range(4):
        for i in (2 * s, 2 * s + 1):
            k, t = ARRIVAL[i]
            if k == 0:
                x_local(t).wait()
                x_arrived(0, t, other).wait_recv()
            else:
                for who in range(2):
                    x_arrived(k, t, who).wait_recv()
            if k == 3:
                x_pass(1, t).start()
            if k == 1:
                x_pass(0, t).start()
        for i in (2 * s, 2 * s + 1):
            turn_block(i)
        for j in range(early):
            if s == 0:
                dy_load(j).wait()
                dy_arrived(j).wait_recv()
            product(2 * s, 2, j)
            for i in (2 * s, 2 * s + 1):
                k, t = ARRIVAL[i]
                near = (k + c - d + nd) % nd
                for when, m in ((2, 0 if t else 1), (3 if t else 1, 3 if t else 2)):
                    @pl.when(near == when)
                    def _(m=m, j=j):
                        y_msg(m, j).start()

    def refill(j):
        if j < len(chunks):
            dy_arrived(j).wait_recv()
            dy_load(j).start()
            dyo_load(j).start()

    refill(2)
    refill(3)
    for j in range(early, len(chunks)):
        dy_load(j).wait()
        dyo_load(j).wait()
        product(0, 4, j)
        product(4, 4, j)
        for m in range(4):
            y_msg(m, j).start()
        refill(j + 2)

    w_swap().wait_recv()
    steps = cols // DEPTH
    rest = cols - steps * DEPTH

    def dx_loads(slot, lo, w):
        at, to = pl.ds(lo, w), pl.ds(pl.multiple_of(slot * DEPTH, DEPTH), w)
        return (lcopy(w_ref.at[:, at], buf.at[0, mine, to], loc_w.at[slot, 0]),
                lcopy(wo.at[:, at], buf.at[0, theirs, to], loc_w.at[slot, 1]),
                lcopy(dy_ref.at[:, at], buf.at[1, pl.ds(0, tokens), to], loc_w.at[slot, 2]))

    quarter = acc.shape[3]
    deep = acc.shape[2]

    def dx_product(slot, w, fresh):
        to = pl.ds(pl.multiple_of(slot * DEPTH, DEPTH), w)

        def step(b, _):
            k, h = b // 2, b % 2
            rows = pl.multiple_of((c + k) % nc * quarter + h * TILE, TILE)
            cut = pl.ds(pl.multiple_of(h * TILE, TILE), TILE)
            for t in range(2):
                out = lax.dot_general(buf[1, t * deep:(t + 1) * deep, to], buf[0, pl.ds(rows, TILE), to],
                                      (((1,), (1,)), ((), ())), preferred_element_type=F32)
                if fresh:
                    acc[k, t, :, cut] = out
                else:
                    acc[k, t, :, cut] += out
            return 0

        lax.fori_loop(0, nc * quarter // TILE, step, 0)

    def dx_at(i):
        return pl.multiple_of(i * DEPTH, 128)

    for copy in dx_loads(0, steps * DEPTH, rest) + dx_loads(1, dx_at(0), DEPTH):
        copy.start()
    for copy in dx_loads(0, steps * DEPTH, rest):
        copy.wait()
    dx_product(0, rest, True)

    def dx_step(i, _):
        slot = (i + 1) % 2

        @pl.when(i + 1 < steps)
        def _():
            for copy in dx_loads(i % 2, dx_at(i + 1), DEPTH):
                copy.start()

        for copy in dx_loads(slot, dx_at(i), DEPTH):
            copy.wait()
        dx_product(slot, DEPTH, False)
        return 0

    lax.fori_loop(0, steps, dx_step, 0)
    for m in range(4):
        x_msg(m).start()

    def pass_y(j):
        at = pl.ds(*chunks[j])
        for down, k, t in ((0, 1, 1), (1, 3, 0)):
            y_msg(down, j).wait_recv()
            part[k, t, :, at] += relay_y[down, :, at]
            y_msg(4 + down, j).start()

    def pass_x():
        for down, k, t in ((0, 1, 1), (1, 3, 0)):
            x_msg(down).wait_recv()
            acc[k, t] += relay_x[down]
            x_msg(4 + down).start()

    for j in range(len(chunks) - 1):
        pass_y(j)
    pass_x()
    pass_y(len(chunks) - 1)

    def done_x():
        for t in range(2):
            for m in ((2, 5) if t == 0 else (3, 4)):
                x_msg(m).wait_recv()
            rows = pl.ds(t * deep, deep)
            buf[1, rows, 0:quarter] = (acc[0, t] + tail_x[t, 0] + tail_x[t, 1]).astype(BF16)
            lcopy(buf.at[1, rows, pl.ds(0, quarter)], dx_ref.at[rows], loc_dx.at[t]).start()

    def done_y(j):
        lo, w = chunks[j]
        at = pl.ds(lo, w)
        for m in range(2, 6):
            y_msg(m, j).wait_recv()
        loads = [lcopy(tail_y.at[t, down, :, at], stage.at[t, down, :, pl.ds(0, w)], loc_s.at[t, down])
                 for t in range(2) for down in range(2)]
        for copy in loads:
            copy.start()
        for copy in loads:
            copy.wait()
        for t in range(2):
            part[0, t, :, at] += stage[t, 0, :, 0:w] + stage[t, 1, :, 0:w]
            out_y(t, j).start()

    def out_y(t, j):
        at = pl.ds(*chunks[j])
        return lcopy(part.at[0, t, :, at], dw_ref.at[pl.ds(t * half, half), at], loc_o.at[t, j])

    done_y(0)
    done_x()
    for j in range(1, len(chunks)):
        done_y(j)

    for t in range(2):
        x_partner(t).wait_send()
        for up in range(2):
            x_pass(up, t).wait_send()
            for core in range(2):
                x_send(up, core, t).wait_send()
        rows = pl.ds(t * deep, deep)
        lcopy(buf.at[1, rows, pl.ds(0, quarter)], dx_ref.at[rows], loc_dx.at[t]).wait()
    w_swap().wait_send()
    for m in range(6):
        x_msg(m).wait_send()
    for j in range(len(chunks)):
        dy_swap(j).wait_send()
        for m in range(6):
            y_msg(m, j).wait_send()
        for t in range(2):
            out_y(t, j).wait()


def solution(mesh):
    act_spec = P(("pod", "data", "row"), "col")
    wgt_spec = P(("pod", "row"), "col")
    nd, nc = mesh.shape["data"], mesh.shape["col"]

    def local_step(x_blk, w_blk, dy_blk):
        tokens, feats = x_blk.shape
        cols = dy_blk.shape[1]
        deep = w_blk.shape[0] * 2 // nd // 2
        half = deep // 2
        count = pl.cdiv(cols, WIDE)
        any_spec = pl.BlockSpec(memory_space=pl.ANY)
        dma = pltpu.SemaphoreType.DMA
        outs = pl.pallas_call(
            functools.partial(kernel, nd, nc),
            out_shape=(
                jax.ShapeDtypeStruct((tokens, feats), BF16),
                jax.ShapeDtypeStruct((deep, cols), F32),
                jax.ShapeDtypeStruct((tokens, cols), BF16),
                jax.ShapeDtypeStruct(w_blk.shape, BF16),
                jax.ShapeDtypeStruct((2, 2, half, cols), F32),
            ),
            in_specs=[any_spec] * 3,
            out_specs=(any_spec,) * 5,
            scratch_shapes=[
                pltpu.VMEM((4, 2, 2 * tokens, half), BF16),
                pltpu.VMEM((8, half, 2 * tokens), BF16),
                pltpu.VMEM((4, 2, half, cols), F32),
                pltpu.VMEM((2, half, cols), F32),
                pltpu.VMEM((4, 2, tokens // 2, feats), F32),
                pltpu.VMEM((2, tokens // 2, feats), F32),
                pltpu.VMEM((2, 2, tokens // 2, feats), F32),
                pltpu.VMEM((2, 2 * tokens, WIDE), BF16),
                pltpu.VMEM((2, 2, half, WIDE), F32),
                dma((2, 2, 2)), dma((4, 2, 2)), dma((2,)), dma((2, 2)), dma((2,)),
                dma((count,)), dma((count,)), dma(()), dma(()), dma((2, 2)),
                dma((6, count)), dma((6, count)), dma((6,)), dma((6,)),
                dma((2, 2)), dma((2, count)), dma((2, 3)), dma((2,)),
            ],
            compiler_params=pltpu.CompilerParams(
                collective_id=0, has_side_effects=True, vmem_limit_bytes=67043328),
        )(x_blk, w_blk, dy_blk)
        return outs[0], outs[1]

    return jax.shard_map(local_step, mesh=mesh, in_specs=(act_spec, wgt_spec, act_spec),
                         out_specs=(act_spec, act_spec), check_vma=False)
```

time: 412 us -> 217 us (0.53)
  the two profiles are of different devices: /device:TPU:97 before, /device:TPU:102 now
where the time goes in v1:
time: 217 us; the launch traced here: 216 us
  Pallas kernels  208 us (96%)
  local copies, waits for them, and re-layouts  7.71 us (4%)
    pallas_call x1, Pallas kernels, local_step(): pl.pallas_call(functools.partial(kernel, nd, nc), out_shape=(jax.ShapeDty...  208 us
    unnamed x2, local copies, waits for them, and re-layouts  7.71 us

profile of v1, /device:TPU:102, one launch (start us, length us, event | category | flops | bytes accessed | tf_op | source)
XLA Modules:
  0.0 216.2 jit_solution(1414994578402942695)
XLA Ops:
  0.6 207.9 %shard_map.50 = (bf16[1024,512]{1,0:T(8,128)(2,1)}, f32[256,5504]{1,0:T(8,128)}, bf16[1024,5504]{1,0:T(8,128)(2,1)}, bf16[1024,5504]{1,0:T(8,128)(2,1)}, f32[2,2,128,5504]{3,2,1,0:T(8,128)}) custom-call(bf16[1024,512]{1,0:T(8,128)(2,1)} %x_ref.1, bf16[1024,5504]{1,0:T(8,128)(2,1)} %w_ref.1, bf16[1024,5504]{1,0:T(8,128)(2,1)} %dy_ref.1), custom_call_target="tpu_custom_call" | custom-call | tf_op jit(solution)/shard_map/pallas_call | solution.py:333
  208.5 2.3 %copy.7 = bf16[1024,512]{1,0:T(8,128)(2,1)} copy(bf16[1024,512]{1,0:T(8,128)(2,1)} %get-tuple-element.8) | data formatting | bytes 2097152
  210.8 5.4 %copy.8 = f32[256,5504]{1,0:T(8,128)} copy(f32[256,5504]{1,0:T(8,128)} %get-tuple-element.9) | data formatting | bytes 11272192

commit v2 on v1

v2 whole, which is shorter than its diff:
```python
import functools

import jax
import jax.numpy as jnp
from jax import lax
from jax.experimental import pallas as pl
from jax.experimental.pallas import tpu as pltpu
from jax.sharding import PartitionSpec as P

MESH = pl.DeviceIdType.MESH
F32, BF16 = jnp.float32, jnp.bfloat16

ARRIVAL = ((0, 0), (0, 1), (1, 0), (3, 1), (1, 1), (3, 0), (2, 0), (2, 1))
WIDE = 1024
TILE = 256
DEPTH = 512


def split(cols):
    widths = [WIDE // 2] + [WIDE] * ((cols - WIDE // 2) // WIDE)
    rest = cols - sum(widths)
    widths += [WIDE // 2] * (rest > WIDE // 2) + [rest - WIDE // 2 * (rest > WIDE // 2)]
    return [(sum(widths[:i]), w) for i, w in enumerate(widths)]


def kernel(nd, nc, x_ref, w_ref, dy_ref, dx_ref, dw_ref, dyo, wo, tail_y,
           xl, xs, xt, part, relay_y, acc, relay_x, tail_x, buf, stage,
           sem_g, rem_g, sem_gp, sem_gf, loc_x, sem_a, rem_a, sem_v, rem_v, sem_w, rem_w, loc_d,
           sem_y, rem_y, sem_x, rem_x, loc_s, loc_o, loc_w, loc_dx):
    d, c, r = lax.axis_index("data"), lax.axis_index("col"), lax.axis_index("row")
    tokens, cols = dy_ref.shape
    half = xt.shape[1]
    piece = half // 2
    band = 2 * half
    d_up, d_dn = (d + 1) % nd, (d + nd - 1) % nd
    c_up, c_dn = (c + 1) % nc, (c + nc - 1) % nc
    other = 1 - r
    mine = pl.ds(pl.multiple_of(r * tokens, tokens), tokens)
    theirs = pl.ds(pl.multiple_of(other * tokens, tokens), tokens)
    chunks = split(cols)
    n = len(chunks)

    def rcopy(src, dst, send, recv, **to):
        return pltpu.make_async_remote_copy(src_ref=src, dst_ref=dst, send_sem=send, recv_sem=recv,
                                            device_id=to, device_id_type=MESH)

    def lcopy(src, dst, sem):
        return pltpu.make_async_copy(src, dst, sem)

    place = {block: i for i, block in enumerate(ARRIVAL)}

    def x_partner(t):
        return rcopy(xs.at[pl.ds(pl.multiple_of(other * band + t * half, half), half)], xt.at[place[0, t], :, mine],
                     sem_gp.at[t], rem_g.at[place[0, t], 0, r], row=other)

    def x_send(up, core, t, p):
        i = place[3 if up else 1, t]
        return rcopy(xs.at[pl.ds(core * band + t * half + p * piece, piece)], xt.at[i, pl.ds(p * piece, piece), mine],
                     sem_g.at[up, core, t, p], rem_g.at[i, p, r], col=c_up if up else c_dn, row=core)

    def x_pass(up, t):
        k, rows, who = (3, pl.ds(0, tokens), 0) if up else (1, pl.ds(tokens, tokens), 1)
        return rcopy(xt.at[place[k, t], :, rows], xt.at[place[2, t], :, rows], sem_gf.at[up, t],
                     rem_g.at[place[2, t], 0, who], col=c_up if up else c_dn)

    def x_arrived(i, p, who):
        k = ARRIVAL[i][0]
        cut = pl.ds(p * piece, piece) if k in (1, 3) else pl.ds(0, half)
        at = xt.at[i, cut, pl.ds(pl.multiple_of(who * tokens, tokens), tokens)]
        return rcopy(at, at, sem_gp.at[0], rem_g.at[i, p, who], row=other)

    def dy_swap(j):
        at = pl.ds(*chunks[j])
        return rcopy(dy_ref.at[:, at], dyo.at[:, at], sem_a.at[j], rem_a.at[j], row=other)

    def dy_direct(j, to):
        lo, w = chunks[j]
        return rcopy(dy_ref.at[:, pl.ds(lo, w)], buf.at[j, to, pl.ds(0, w)], sem_v.at[j], rem_v.at[j], row=other)

    def dy_load(j):
        lo, w = chunks[j]
        return lcopy(dy_ref.at[:, pl.ds(lo, w)], buf.at[j % 2, mine, pl.ds(0, w)], loc_d.at[j % 2, 0])

    def dyo_load(j):
        lo, w = chunks[j]
        return lcopy(dyo.at[:, pl.ds(lo, w)], buf.at[j % 2, theirs, pl.ds(0, w)], loc_d.at[j % 2, 1])

    def w_swap():
        return rcopy(w_ref, wo, sem_w, rem_w, row=other)

    def y_msg(m, j, p):
        at = pl.ds(*chunks[j])
        k, t = ((2, 1), (2, 0), (1, 0), (3, 1), (1, 1), (3, 0))[m]
        rows = pl.ds(p * piece, piece)
        down = m % 2
        dst = relay_y.at[down, rows, at] if m < 2 else tail_y.at[t, down, rows, at]
        return rcopy(part.at[k, t, rows, at], dst, sem_y.at[m, j, p], rem_y.at[m, j, p], data=d_dn if down else d_up)

    def x_msg(m):
        k, t = ((2, 1), (2, 0), (1, 0), (3, 1), (1, 1), (3, 0))[m]
        down = m % 2
        dst = relay_x.at[down] if m < 2 else tail_x.at[t, down]
        return rcopy(acc.at[k, t], dst, sem_x.at[m], rem_x.at[m], col=c_dn if down else c_up)

    x_load = lcopy(x_ref, xl, loc_x)
    x_load.start()
    for j in range(2):
        dy_load(j).start()

    barrier = pltpu.get_barrier_semaphore()
    peers = [dict(row=other), dict(data=d_up), dict(data=d_dn)]
    peers += [dict(col=n, row=k) for n in (c_up, c_dn) for k in range(2)]
    for peer in peers:
        pl.semaphore_signal(barrier, inc=1, device_id=peer, device_id_type=MESH)
    x_load.wait()
    for b in range(xl.shape[1] // 128):
        xs[b * 128:(b + 1) * 128, :] = xl[:, b * 128:(b + 1) * 128].T
    for t in range(2):
        xt[place[0, t], :, mine] = xs[pl.ds(pl.multiple_of(r * band + t * half, half), half), :]
    pl.semaphore_wait(barrier, len(peers))

    for p in range(2):
        for core in range(2):
            x_send(1, core, 1, p).start()
            x_send(0, core, 0, p).start()
        if p == 0:
            for t in range(2):
                x_partner(t).start()
            dy_direct(0, mine).start()
    for p in range(2):
        for core in range(2):
            x_send(1, core, 0, p).start()
            x_send(0, core, 1, p).start()
    dy_direct(1, mine).start()
    for j in (*range(2, n), 0, 1):
        dy_swap(j).start()
    w_swap().start()

    def product(first, count, j, lead=0, rows=half):
        lo, w = chunks[j]

        def one(at, width):
            lhs = xt[first:first + count, lead:lead + rows].reshape(count * rows, 2 * tokens)
            rhs = buf[j % 2, :, pl.ds(at, width)]
            out = lax.dot_general(lhs, rhs, (((1,), (0,)), ((), ())), preferred_element_type=F32)
            for i in range(count):
                k, t = ARRIVAL[first + i]
                part[(k + c - d + nd) % nd, t, lead:lead + rows, pl.ds(pl.multiple_of(lo + at, 128), width)] = out[i * rows:(i + 1) * rows]

        def step(b, _):
            one(pl.multiple_of(b * TILE, TILE), TILE)
            return 0

        lax.fori_loop(0, w // TILE, step, 0)
        if w % TILE:
            one(w - w % TILE, w % TILE)

    def send(first, count, j, pieces):
        for k, t in ARRIVAL[first:first + count]:
            near = (k + c - d + nd) % nd
            for when, m in ((2, 0 if t else 1), (3 if t else 1, 3 if t else 2)):
                @pl.when(near == when)
                def _(m=m):
                    for p in pieces:
                        y_msg(m, j, p).start()

    swapped = set()

    def refill(j):
        if j not in swapped:
            dy_swap(j).wait_recv()
            swapped.add(j)
        dy_load(j).start()
        dyo_load(j).start()

    def filled(j):
        dy_load(j).wait()
        dyo_load(j).wait()

    for t in range(2):
        x_arrived(place[0, t], 0, other).wait_recv()
    for j in range(2):
        dy_load(j).wait()
        dy_direct(j, theirs).wait_recv()
        product(0, 2, j)
        send(0, 2, j, (0, 1))
        if j == 0:
            for i in (2, 3):
                for who in range(2):
                    x_arrived(i, 0, who).wait_recv()
        product(2, 2, j, 0, piece)
        send(2, 2, j, (0,))
    for i in (2, 3):
        for who in range(2):
            x_arrived(i, 1, who).wait_recv()
    x_pass(1, 1).start()
    x_pass(0, 0).start()
    for j in range(2):
        product(2, 2, j, piece, piece)
        send(2, 2, j, (1,))
        refill(j + 2)
    for j in range(2, n):
        filled(j)
        product(0, 4, j)
        send(0, 4, j, (0, 1))
        if j + 2 < n:
            refill(j + 2)
    for i in (4, 5):
        for p in range(2):
            for who in range(2):
                x_arrived(i, p, who).wait_recv()
    x_pass(1, 0).start()
    x_pass(0, 1).start()
    refill(0)
    refill(1)
    for i in (6, 7):
        for who in range(2):
            x_arrived(i, 0, who).wait_recv()

    for j in range(n):
        filled(j)
        product(4, 4, j)
        send(4, 4, j, (0, 1))
        if j + 2 < n:
            refill(j + 2)

    w_swap().wait_recv()
    steps = cols // DEPTH
    rest = cols - steps * DEPTH

    def dx_loads(slot, lo, w):
        at, to = pl.ds(lo, w), pl.ds(pl.multiple_of(slot * DEPTH, DEPTH), w)
        return (lcopy(w_ref.at[:, at], buf.at[0, mine, to], loc_w.at[slot, 0]),
                lcopy(wo.at[:, at], buf.at[0, theirs, to], loc_w.at[slot, 1]),
                lcopy(dy_ref.at[:, at], buf.at[1, pl.ds(0, tokens), to], loc_w.at[slot, 2]))

    quarter = acc.shape[3]
    deep = acc.shape[2]

    def dx_product(slot, w, fresh):
        to = pl.ds(pl.multiple_of(slot * DEPTH, DEPTH), w)

        def step(b, _):
            k, h = b // 2, b % 2
            rows = pl.multiple_of((c + k) % nc * quarter + h * TILE, TILE)
            cut = pl.ds(pl.multiple_of(h * TILE, TILE), TILE)
            for t in range(2):
                out = lax.dot_general(buf[1, t * deep:(t + 1) * deep, to], buf[0, pl.ds(rows, TILE), to],
                                      (((1,), (1,)), ((), ())), preferred_element_type=F32)
                if fresh:
                    acc[k, t, :, cut] = out
                else:
                    acc[k, t, :, cut] += out
            return 0

        lax.fori_loop(0, nc * quarter // TILE, step, 0)

    def dx_at(i):
        return pl.multiple_of(i * DEPTH, 128)

    for copy in dx_loads(0, steps * DEPTH, rest) + dx_loads(1, dx_at(0), DEPTH):
        copy.start()
    for copy in dx_loads(0, steps * DEPTH, rest):
        copy.wait()
    dx_product(0, rest, True)

    def dx_step(i, _):
        slot = (i + 1) % 2

        @pl.when(i + 1 < steps)
        def _():
            for copy in dx_loads(i % 2, dx_at(i + 1), DEPTH):
                copy.start()

        for copy in dx_loads(slot, dx_at(i), DEPTH):
            copy.wait()
        dx_product(slot, DEPTH, False)
        return 0

    lax.fori_loop(0, steps, dx_step, 0)
    for m in range(4):
        x_msg(m).start()

    def pass_y(j):
        at = pl.ds(*chunks[j])
        for down, k, t in ((0, 1, 1), (1, 3, 0)):
            for p in range(2):
                rows = slice(p * piece, (p + 1) * piece)
                y_msg(down, j, p).wait_recv()
                part[k, t, rows, at] += relay_y[down, rows, at]
                y_msg(4 + down, j, p).start()

    def pass_x():
        for down, k, t in ((0, 1, 1), (1, 3, 0)):
            x_msg(down).wait_recv()
            acc[k, t] += relay_x[down]
            x_msg(4 + down).start()

    for j in range(n):
        pass_y(j)
    pass_x()

    def done_x():
        for t in range(2):
            for m in ((2, 5) if t == 0 else (3, 4)):
                x_msg(m).wait_recv()
            rows = pl.ds(t * deep, deep)
            buf[1, rows, 0:quarter] = (acc[0, t] + tail_x[t, 0] + tail_x[t, 1]).astype(BF16)
            lcopy(buf.at[1, rows, pl.ds(0, quarter)], dx_ref.at[rows], loc_dx.at[t]).start()

    def done_y(j):
        lo, w = chunks[j]
        at = pl.ds(lo, w)
        for m in range(2, 6):
            for p in range(2):
                y_msg(m, j, p).wait_recv()
        if j == len(chunks) - 1:
            return
        loads = [lcopy(tail_y.at[t, down, :, at], stage.at[t, down, :, pl.ds(0, w)], loc_s.at[t, down])
                 for t in range(2) for down in range(2)]
        for copy in loads:
            copy.start()
        for copy in loads:
            copy.wait()
        for t in range(2):
            part[0, t, :, at] += stage[t, 0, :, 0:w] + stage[t, 1, :, 0:w]
            out_y(t, j).start()

    def out_y(t, j):
        at = pl.ds(*chunks[j])
        return lcopy(part.at[0, t, :, at], dw_ref.at[pl.ds(t * half, half), at], loc_o.at[t, j])

    for t in range(2):
        out_y(t, len(chunks) - 1).start()
    done_x()
    for j in range(n):
        done_y(j)

    for t in range(2):
        x_partner(t).wait_send()
        for up in range(2):
            x_pass(up, t).wait_send()
            for core in range(2):
                for p in range(2):
                    x_send(up, core, t, p).wait_send()
        rows = pl.ds(t * deep, deep)
        lcopy(buf.at[1, rows, pl.ds(0, quarter)], dx_ref.at[rows], loc_dx.at[t]).wait()
    w_swap().wait_send()
    for m in range(6):
        x_msg(m).wait_send()
    for j in range(len(chunks)):
        dy_swap(j).wait_send()
        if j < 2:
            dy_direct(j, mine).wait_send()
        for m in range(6):
            for p in range(2):
                y_msg(m, j, p).wait_send()
        for t in range(2):
            out_y(t, j).wait()


def finish(last, dx_in, dw_in, tail, dx_ref, dw_ref, dx_v, dw_v, tail_v, sem_in, sem_out, sem_t):
    deep, cols = dw_in.shape
    rows = deep // PARTS
    left = cols - last
    front, back = pl.ds(0, last), pl.ds(last, left)

    def piece(i):
        if i < PARTS:
            at = pl.ds(i * rows, rows)
            return dw_in.at[at, front], dw_v.at[at, front], dw_ref.at[at, front]
        if i == PARTS:
            return dw_in.at[:, back], dw_v.at[:, back], dw_ref.at[:, back]
        return dx_in, dx_v, dx_ref

    def load(i):
        src, mid, _ = piece(i)
        return pltpu.make_async_copy(src, mid, sem_in.at[i])

    def store(i):
        _, mid, dst = piece(i)
        return pltpu.make_async_copy(mid, dst, sem_out.at[i])

    tails = pltpu.make_async_copy(tail.at[:, :, :, back], tail_v, sem_t)
    order = (*range(PARTS), PARTS + 1, PARTS)
    tails.start()
    for i in (PARTS, *range(PARTS), PARTS + 1):
        load(i).start()
    for i in order:
        load(i).wait()
        if i == PARTS:
            tails.wait()
            for t in range(2):
                at = slice(t * (deep // 2), (t + 1) * (deep // 2))
                dw_v[at, last:] += tail_v[t, 0] + tail_v[t, 1]
        store(i).start()
    for i in order:
        store(i).wait()


PARTS = 8


def solution(mesh):
    act_spec = P(("pod", "data", "row"), "col")
    wgt_spec = P(("pod", "row"), "col")
    nd, nc = mesh.shape["data"], mesh.shape["col"]

    def local_step(x_blk, w_blk, dy_blk):
        tokens, feats = x_blk.shape
        cols = dy_blk.shape[1]
        deep = w_blk.shape[0] * 2 // nd // 2
        half = deep // 2
        count = len(split(cols))
        any_spec = pl.BlockSpec(memory_space=pl.ANY)
        dma = pltpu.SemaphoreType.DMA
        outs = pl.pallas_call(
            functools.partial(kernel, nd, nc),
            out_shape=(
                jax.ShapeDtypeStruct((tokens, feats), BF16),
                jax.ShapeDtypeStruct((deep, cols), F32),
                jax.ShapeDtypeStruct((tokens, cols), BF16),
                jax.ShapeDtypeStruct(w_blk.shape, BF16),
                jax.ShapeDtypeStruct((2, 2, half, cols), F32),
            ),
            in_specs=[any_spec] * 3,
            out_specs=(any_spec,) * 5,
            scratch_shapes=[
                pltpu.VMEM((tokens, feats), BF16),
                pltpu.VMEM((feats, tokens), BF16),
                pltpu.VMEM((8, half, 2 * tokens), BF16),
                pltpu.VMEM((4, 2, half, cols), F32),
                pltpu.VMEM((2, half, cols), F32),
                pltpu.VMEM((4, 2, tokens // 2, feats), F32),
                pltpu.VMEM((2, tokens // 2, feats), F32),
                pltpu.VMEM((2, 2, tokens // 2, feats), F32),
                pltpu.VMEM((2, 2 * tokens, WIDE), BF16),
                pltpu.VMEM((2, 2, half, WIDE), F32),
                dma((2, 2, 2, 2)), dma((8, 2, 2)), dma((2,)), dma((2, 2)), dma(()),
                dma((count,)), dma((count,)), dma((2,)), dma((2,)), dma(()), dma(()), dma((2, 2)),
                dma((6, count, 2)), dma((6, count, 2)), dma((6,)), dma((6,)),
                dma((2, 2)), dma((2, count)), dma((2, 3)), dma((2,)),
            ],
            compiler_params=pltpu.CompilerParams(
                collective_id=0, has_side_effects=True, vmem_limit_bytes=67043328),
        )(x_blk, w_blk, dy_blk)
        last = split(cols)[-1][0]
        return pl.pallas_call(
            functools.partial(finish, last),
            out_shape=(
                jax.ShapeDtypeStruct((tokens, feats), BF16),
                jax.ShapeDtypeStruct((deep, cols), F32),
            ),
            in_specs=[any_spec] * 3,
            out_specs=(any_spec,) * 2,
            scratch_shapes=[
                pltpu.VMEM((tokens, feats), BF16),
                pltpu.VMEM((deep, cols), F32),
                pltpu.VMEM((2, 2, half, cols - last), F32),
                dma((PARTS + 2,)), dma((PARTS + 2,)), dma(()),
            ],
            compiler_params=pltpu.CompilerParams(vmem_limit_bytes=67043328),
        )(outs[0], outs[1], outs[4])

    return jax.shard_map(local_step, mesh=mesh, in_specs=(act_spec, wgt_spec, act_spec),
                         out_specs=(act_spec, act_spec), check_vma=False)
```

time: 217 us -> 207 us (0.954)
  the two profiles are of different devices: /device:TPU:102 before, /device:TPU:97 now
where the time goes in v2:
time: 207 us
  Pallas kernels  206 us (100%)
    pallas_call x1, Pallas kernels, local_step(): pl.pallas_call(functools.partial(kernel, nd, nc), out_shape=(jax.ShapeDty...  200 us
    pallas_call x1, Pallas kernels, local_step(): pl.pallas_call(functools.partial(finish, last), out_shape=(jax.ShapeDtype...  6.31 us

profile of v2, /device:TPU:97, one launch (start us, length us, event | category | flops | bytes accessed | tf_op | source)
XLA Modules:
  0.0 206.8 jit_solution(8083145607688563404)
XLA Ops:
  0.6 199.7 %shard_map.50 = (bf16[1024,512]{1,0:T(8,128)(2,1)}, f32[256,5504]{1,0:T(8,128)}, bf16[1024,5504]{1,0:T(8,128)(2,1)}, bf16[1024,5504]{1,0:T(8,128)(2,1)}, f32[2,2,128,5504]{3,2,1,0:T(8,128)}) custom-call(bf16[1024,512]{1,0:T(8,128)(2,1)} %x_ref.1, bf16[1024,5504]{1,0:T(8,128)(2,1)} %w_ref.1, bf16[1024,5504]{1,0:T(8,128)(2,1)} %dy_ref.1), custom_call_target="tpu_custom_call" | custom-call | tf_op jit(solution)/shard_map/pallas_call | solution.py:417
  200.3 6.3 %shard_map.51 = (bf16[1024,512]{1,0:T(8,128)(2,1)}, f32[256,5504]{1,0:T(8,128)}) custom-call(bf16[1024,512]{1,0:T(8,128)(2,1)} %get-tuple-element.5.dx_in, f32[256,5504]{1,0:T(8,128)} %get-tuple-element.6.dw_in, f32[2,2,128,5504]{3,2,1,0:T(8,128)} %get-tuple-element.7.tail), custom_call_target="tpu_custom_call" | custom-call | tf_op jit(solution)/shard_map/pallas_call | solution.py:448

commit v3 on v0

v3 whole, which is shorter than its diff:
```python
import functools

import jax
import jax.numpy as jnp
from jax import lax
from jax.experimental import pallas as pl
from jax.experimental.pallas import tpu as pltpu
from jax.sharding import PartitionSpec as P

MESH = pl.DeviceIdType.MESH
F32, BF16 = jnp.float32, jnp.bfloat16

TILE = 256
DEPTH = 512
PARTS = 8


def pieces(width):
    return [(lo, min(DEPTH, width - lo)) for lo in range(0, width, DEPTH)]


def kernel(nd, nc, x_ref, w_ref, dy_ref, dx_ref, dw_ref, dyo, wo, nbr,
           xl, xs, xt, part, own, relay_y, tail_y, acc, relay_x, tail_x, buf,
           sem_p, sem_g, sem_r, rem_g, sem_h, rem_h, sem_f, loc_x, sem_a, rem_a, sem_w, rem_w,
           sem_n, rem_n, sem_s, rem_s, loc_d, loc_n, sem_y, rem_y, sem_x, rem_x, loc_o, loc_w, loc_dx):
    d, c, r = lax.axis_index("data"), lax.axis_index("col"), lax.axis_index("row")
    tokens, cols = dy_ref.shape
    band = xt.shape[2]
    span = own.shape[2]
    d_up, d_dn = (d + 1) % nd, (d + nd - 1) % nd
    c_up, c_dn = (c + 1) % nc, (c + nc - 1) % nc
    other = 1 - r
    mine = pl.ds(pl.multiple_of(r * tokens, tokens), tokens)
    theirs = pl.ds(pl.multiple_of(other * tokens, tokens), tokens)
    subs = pieces(span)
    n = len(subs)

    def rcopy(src, dst, send, recv, **to):
        return pltpu.make_async_remote_copy(src_ref=src, dst_ref=dst, send_sem=send, recv_sem=recv,
                                            device_id=to, device_id_type=MESH)

    def lcopy(src, dst, sem):
        return pltpu.make_async_copy(src, dst, sem)

    def near(k):
        return (k + c - d + nd) % nd

    def start_of(e):
        k = (d + e) % nd
        return k * span - k // (nd - 1) * (nd * span - cols)

    def cut(e, j):
        lo, w = subs[j]
        return pl.ds(pl.multiple_of(start_of(e) + lo, 128), w)

    def rows_for(core):
        return xs.at[pl.ds(pl.multiple_of(core * band, band), band)]

    def x_partner():
        return rcopy(rows_for(other), xt.at[0, 0, :, mine], sem_p, rem_g.at[0, 0, r], row=other)

    def x_side(up, core):
        k = 3 if up else 1
        return rcopy(rows_for(core), xt.at[0, k, :, mine], sem_g.at[up, core], rem_g.at[0, k, r],
                     col=c_up if up else c_dn, row=core)

    def x_rows(up, core):
        row = 2 if up else 1
        return rcopy(rows_for(core), xt.at[row, 0, :, mine], sem_r.at[up, core], rem_g.at[row, 0, r],
                     data=d_up if up else d_dn, row=core)

    def x_next(row, up):
        return rcopy(xt.at[row, 0], xt.at[row, 3 if up else 1], sem_h.at[row - 1, up], rem_h.at[row - 1, up],
                     col=c_up if up else c_dn)

    def x_pass(row, up):
        who = 0 if up else 1
        at = pl.ds(who * tokens, tokens)
        return rcopy(xt.at[row, 3 if up else 1, :, at], xt.at[row, 2, :, at], sem_f.at[row, up], rem_g.at[row, 2, who],
                     col=c_up if up else c_dn)

    def x_arrived(row, k, who):
        at = xt.at[row, k, :, pl.ds(pl.multiple_of(who * tokens, tokens), tokens)]
        return rcopy(at, at, sem_p, rem_g.at[row, k, who], row=other)

    def dy_swap():
        return rcopy(dy_ref, dyo, sem_a, rem_a, row=other)

    soon = cols // DEPTH * 2 // 5
    halves = ((0, soon * DEPTH), (soon * DEPTH, cols - soon * DEPTH))

    def w_swap(i):
        at = pl.ds(*halves[i])
        return rcopy(w_ref.at[:, at], wo.at[:, at], sem_w.at[i], rem_w.at[i], row=other)

    def dy_give(down, j):
        return rcopy(dy_ref.at[:, cut(down, j)], nbr.at[down, mine, pl.ds(*subs[j])], sem_n.at[down, j], rem_n.at[down, j],
                     data=d_dn if down else d_up)

    def dy_share(i, j, rows):
        at = nbr.at[i, rows, pl.ds(*subs[j])]
        return rcopy(at, at, sem_s.at[i, j], rem_s.at[i, j], row=other)

    def y_msg(m, j):
        at = pl.ds(*subs[j])
        i, k = ((0, 2), (1, 2), (0, 1), (1, 3), (1, 1), (0, 3))[m]
        down = m % 2
        dst = relay_y.at[down, :, at] if m < 2 else tail_y.at[(1, 0, 3, 2)[m - 2], :, at]
        return rcopy(part.at[i, k, :, at], dst, sem_y.at[m, j], rem_y.at[m, j], data=d_dn if down else d_up)

    def x_msg(m):
        k, t = ((2, 1), (2, 0), (1, 0), (3, 1), (1, 1), (3, 0))[m]
        down = m % 2
        dst = relay_x.at[down] if m < 2 else tail_x.at[t, down]
        return rcopy(acc.at[k, t], dst, sem_x.at[m], rem_x.at[m], col=c_dn if down else c_up)

    x_load = lcopy(x_ref, xl, loc_x)
    x_load.start()
    barrier = pltpu.get_barrier_semaphore()
    peers = [dict(row=other)]
    peers += [dict(data=k, row=core) for k in (d_up, d_dn) for core in range(2)]
    peers += [dict(col=k, row=core) for k in (c_up, c_dn) for core in range(2)]
    for peer in peers:
        pl.semaphore_signal(barrier, inc=1, device_id=peer, device_id_type=MESH)
    x_load.wait()
    for b in range(xl.shape[1] // 128):
        xs[b * 128:(b + 1) * 128, :] = xl[:, b * 128:(b + 1) * 128].T
    xt[0, 0, :, mine] = xs[pl.ds(pl.multiple_of(r * band, band), band), :]
    pl.semaphore_wait(barrier, len(peers))

    for core in range(2):
        for up in range(2):
            x_rows(up, core).start()
            x_side(up, core).start()
    x_partner().start()
    w_swap(0).start()
    for j in range(n):
        for down in range(2):
            dy_give(down, j).start()
    w_swap(1).start()
    dy_swap().start()

    steps = cols // DEPTH
    rest = cols - steps * DEPTH
    quarter = acc.shape[3]
    deep = acc.shape[2]

    def dx_loads(slot, lo, w):
        at, to = pl.ds(lo, w), pl.ds(pl.multiple_of(slot * DEPTH, DEPTH), w)
        return (lcopy(w_ref.at[:, at], buf.at[0, mine, to], loc_w.at[slot, 0]),
                lcopy(wo.at[:, at], buf.at[0, theirs, to], loc_w.at[slot, 1]),
                lcopy(dy_ref.at[:, at], buf.at[1, pl.ds(0, tokens), to], loc_w.at[slot, 2]))

    def dx_product(slot, w, fresh):
        to = pl.ds(pl.multiple_of(slot * DEPTH, DEPTH), w)

        def step(b, _):
            k, h = b // 2, b % 2
            rows = pl.multiple_of((c + k) % nc * quarter + h * TILE, TILE)
            at = pl.ds(pl.multiple_of(h * TILE, TILE), TILE)
            for t in range(2):
                out = lax.dot_general(buf[1, t * deep:(t + 1) * deep, to], buf[0, pl.ds(rows, TILE), to],
                                      (((1,), (1,)), ((), ())), preferred_element_type=F32)
                if fresh:
                    acc[k, t, :, at] = out
                else:
                    acc[k, t, :, at] += out
            return 0

        lax.fori_loop(0, nc * quarter // TILE, step, 0)

    def dx_run(first, stop, fresh):
        def loads(i):
            return dx_loads(i % 2, pl.multiple_of(i * DEPTH, 128), DEPTH)

        def step(i, clear):
            @pl.when(i + 1 < stop)
            def _():
                for copy in loads(i + 1):
                    copy.start()

            for copy in loads(i):
                copy.wait()
            dx_product(i % 2, DEPTH, clear)

        def body(i, _):
            step(i, False)
            return 0

        for copy in loads(first):
            copy.start()
        if fresh:
            step(jnp.int32(first), True)
        lax.fori_loop(first + fresh, stop, body, 0)

    w_swap(0).wait_recv()
    dx_run(0, soon, 1)
    for k in (1, 3):
        for who in range(2):
            x_arrived(0, k, who).wait_recv()
    for up in range(2):
        x_pass(0, up).start()
    for row in (1, 2):
        for who in range(2):
            x_arrived(row, 0, who).wait_recv()
        for up in range(2):
            x_next(row, up).start()
    w_swap(1).wait_recv()
    dx_run(soon, steps, 0)
    for copy in dx_loads(0, steps * DEPTH, rest):
        copy.start()
    for copy in dx_loads(0, steps * DEPTH, rest):
        copy.wait()
    dx_product(0, rest, False)

    def tiles(w, one):
        def step(b, _):
            one(pl.multiple_of(b * TILE, TILE), TILE)
            return 0

        lax.fori_loop(0, w // TILE, step, 0)
        if w % TILE:
            one(w - w % TILE, w % TILE)

    def dot(lhs, slot, at, width):
        return lax.dot_general(lhs, buf[slot, :, pl.ds(at, width)], (((1,), (0,)), ((), ())), preferred_element_type=F32)

    def heavy(i, j, slot):
        lo, w = subs[j]

        def one(at, width):
            to = pl.ds(pl.multiple_of(lo + at, 128), width)
            for k in (0, 2):
                out = dot(xt[0, k:k + 2].reshape(2 * band, 2 * tokens), slot, at, width)
                part[i, near(k), :, to] = out[:band]
                part[i, near(k + 1), :, to] = out[band:]

        tiles(w, one)

    def light(e, j, slot):
        lo, w = subs[j]

        def one(at, width):
            own[e, :, pl.ds(pl.multiple_of(lo + at, 128), width)] = dot(xt[0, (d - c + nc) % nc], slot, at, width)

        tiles(w, one)

    def own_load(e, j, slot):
        to = pl.ds(0, subs[j][1])
        return (lcopy(dy_ref.at[:, cut(e, j)], buf.at[slot, mine, to], loc_d.at[slot, 0]),
                lcopy(dyo.at[:, cut(e, j)], buf.at[slot, theirs, to], loc_d.at[slot, 1]))

    dy_swap().wait_recv()
    work = [(e, j) for j in range(n) for e in (3, 2)] + [(e, j) for j in range(n) for e in (0, 1)]
    for copy in own_load(*work[0], 0):
        copy.start()
    x_arrived(0, 0, other).wait_recv()
    for who in range(2):
        x_arrived(0, 2, who).wait_recv()
    for i, (e, j) in enumerate(work):
        if i + 1 < len(work):
            for copy in own_load(*work[i + 1], (i + 1) % 2):
                copy.start()
        for copy in own_load(e, j, i % 2):
            copy.wait()
        if e > 1:
            heavy(3 - e, j, i % 2)
        else:
            light(e, j, i % 2)
        if i == n:
            for up in range(2):
                x_next(1, up).wait_recv()
                x_pass(1, up).start()
        if i >= 2 * n and i % 2 and i // 2 - n < n - 1:
            for side in range(2):
                dy_give(side, i // 2 - n).wait_recv()
                dy_share(side, i // 2 - n, mine).start()

    def nbr_load(side, j, slot):
        to = pl.ds(0, subs[j][1])
        return lcopy(nbr.at[side, :, pl.ds(*subs[j])], buf.at[slot, :, to], loc_n.at[slot])

    def add(side, j, slot, ks):
        lo, w = subs[j]
        for k in ks:
            @pl.when(near(k) != (1 if side else 3))
            def _(k=k):
                def one(at, width):
                    to = pl.ds(pl.multiple_of(lo + at, 128), width)
                    part[side, near(k), :, to] += dot(xt[1 if side else 2, k], slot, at, width)

                tiles(w, one)

            for q, m in ((2, side), (3 if side else 1, 2 + side)):
                @pl.when(near(k) == q)
                def _(m=m):
                    y_msg(m, j).start()

    work = [(side, j) for j in range(n) for side in (1, 0)]
    work = [(*item, (0, 3, 1)) for item in work] + [(*item, (2,)) for item in work]
    shared = set()

    def ready(side, j):
        if (side, j) not in shared:
            shared.add((side, j))
            if j == n - 1:
                dy_give(side, j).wait_recv()
                dy_share(side, j, mine).start()
            dy_share(side, j, theirs).wait_recv()

    ready(*work[0][:2])
    nbr_load(*work[0][:2], 0).start()
    for i, (side, j, ks) in enumerate(work):
        if i + 1 < len(work):
            ready(*work[i + 1][:2])
            nbr_load(*work[i + 1][:2], (i + 1) % 2).start()
        nbr_load(side, j, i % 2).wait()
        if i == 1:
            for up in range(2):
                x_next(2, up).wait_recv()
                x_pass(2, up).start()
            for m in range(4):
                x_msg(m).start()
        if i == 2 * n:
            for row in (1, 2):
                for who in range(2):
                    x_arrived(row, 2, who).wait_recv()
        add(side, j, i % 2, ks)

    def pass_y(j):
        at = pl.ds(*subs[j])
        for down, i, k in ((0, 1, 1), (1, 0, 3)):
            y_msg(down, j).wait_recv()
            part[i, k, :, at] += relay_y[down, :, at]
            y_msg(4 + down, j).start()

    def pass_x():
        for down, k, t in ((0, 1, 1), (1, 3, 0)):
            x_msg(down).wait_recv()
            acc[k, t] += relay_x[down]
            x_msg(4 + down).start()

    pass_y(0)
    pass_x()
    for j in range(1, n):
        pass_y(j)

    def mine_of(e):
        return own.at[e] if e < 2 else part.at[3 - e, 0]

    def out_y(e, j):
        return lcopy(mine_of(e).at[:, pl.ds(*subs[j])], dw_ref.at[:, cut(e, j)], loc_o.at[e % 2])

    def done_y(pair):
        for j in range(n):
            at = pl.ds(*subs[j])
            for e in pair:
                y_msg((5, 4, 2, 3)[e], j).wait_recv()
                mine_of(e)[:, at] += tail_y[(2, 3, 1, 0)[e], :, at]
            if j:
                for e in pair:
                    out_y(e, j - 1).wait()
            for e in pair:
                out_y(e, j).start()
        for e in pair:
            out_y(e, n - 1).wait()

    done_y((3, 2))
    for t in range(2):
        for m in ((2, 5) if t == 0 else (3, 4)):
            x_msg(m).wait_recv()
        rows = pl.ds(t * deep, deep)
        buf[1, rows, 0:quarter] = (acc[0, t] + tail_x[t, 0] + tail_x[t, 1]).astype(BF16)
        lcopy(buf.at[1, rows, pl.ds(0, quarter)], dx_ref.at[rows], loc_dx.at[t]).start()
    done_y((0, 1))

    x_partner().wait_send()
    for up in range(2):
        for core in range(2):
            x_side(up, core).wait_send()
            x_rows(up, core).wait_send()
        for row in range(3):
            x_pass(row, up).wait_send()
        for row in (1, 2):
            x_next(row, up).wait_send()
    for t in range(2):
        rows = pl.ds(t * deep, deep)
        lcopy(buf.at[1, rows, pl.ds(0, quarter)], dx_ref.at[rows], loc_dx.at[t]).wait()
        w_swap(t).wait_send()
    dy_swap().wait_send()
    for m in range(6):
        x_msg(m).wait_send()
    for j in range(n):
        for side in range(2):
            dy_give(side, j).wait_send()
            dy_share(side, j, mine).wait_send()
        for m in range(6):
            y_msg(m, j).wait_send()


def finish(dx_in, dw_in, dx_ref, dw_ref, dx_v, dw_v, sem_in, sem_out):
    rows = dw_in.shape[0] // PARTS

    def piece(i):
        if i < PARTS:
            at = pl.ds(i * rows, rows)
            return dw_in.at[at], dw_v.at[at], dw_ref.at[at]
        return dx_in, dx_v, dx_ref

    def load(i):
        return pltpu.make_async_copy(*piece(i)[:2], sem_in.at[i])

    def store(i):
        return pltpu.make_async_copy(*piece(i)[1:], sem_out.at[i])

    for i in range(PARTS + 1):
        load(i).start()
    for i in range(PARTS + 1):
        load(i).wait()
        store(i).start()
    for i in range(PARTS + 1):
        store(i).wait()


def solution(mesh):
    act_spec = P(("pod", "data", "row"), "col")
    wgt_spec = P(("pod", "row"), "col")
    nd, nc, nr = mesh.shape["data"], mesh.shape["col"], mesh.shape["row"]

    def local_step(x_blk, w_blk, dy_blk):
        tokens, feats = x_blk.shape
        cols = dy_blk.shape[1]
        band = feats // nr
        span = pl.cdiv(cols, 128 * nd) * 128
        n = len(pieces(span))
        any_spec = pl.BlockSpec(memory_space=pl.ANY)
        dma = pltpu.SemaphoreType.DMA
        outs = pl.pallas_call(
            functools.partial(kernel, nd, nc),
            out_shape=(
                jax.ShapeDtypeStruct((tokens, feats), BF16),
                jax.ShapeDtypeStruct((band, cols), F32),
                jax.ShapeDtypeStruct((tokens, cols), BF16),
                jax.ShapeDtypeStruct(w_blk.shape, BF16),
                jax.ShapeDtypeStruct((2, 2 * tokens, span), BF16),
            ),
            in_specs=[any_spec] * 3,
            out_specs=(any_spec,) * 5,
            scratch_shapes=[
                pltpu.VMEM((tokens, feats), BF16),
                pltpu.VMEM((feats, tokens), BF16),
                pltpu.VMEM((3, 4, band, 2 * tokens), BF16),
                pltpu.VMEM((2, 4, band, span), F32),
                pltpu.VMEM((2, band, span), F32),
                pltpu.VMEM((2, band, span), F32),
                pltpu.VMEM((4, band, span), F32),
                pltpu.VMEM((4, 2, tokens // 2, feats), F32),
                pltpu.VMEM((2, tokens // 2, feats), F32),
                pltpu.VMEM((2, 2, tokens // 2, feats), F32),
                pltpu.VMEM((2, 2 * tokens, 2 * DEPTH), BF16),
                dma(()), dma((2, 2)), dma((2, 2)), dma((3, 4, 2)), dma((2, 2)), dma((2, 2)), dma((3, 2)), dma(()),
                dma(()), dma(()), dma((2,)), dma((2,)),
                dma((2, n)), dma((2, n)), dma((2, n)), dma((2, n)), dma((2, 2)), dma((2,)),
                dma((6, n)), dma((6, n)), dma((6,)), dma((6,)), dma((2,)), dma((2, 3)), dma((2,)),
            ],
            compiler_params=pltpu.CompilerParams(
                collective_id=0, has_side_effects=True, vmem_limit_bytes=67043328),
        )(x_blk, w_blk, dy_blk)
        return pl.pallas_call(
            finish,
            out_shape=(
                jax.ShapeDtypeStruct((tokens, feats), BF16),
                jax.ShapeDtypeStruct((band, cols), F32),
            ),
            in_specs=[any_spec] * 2,
            out_specs=(any_spec,) * 2,
            scratch_shapes=[
                pltpu.VMEM((tokens, feats), BF16),
                pltpu.VMEM((band, cols), F32),
                dma((PARTS + 1,)), dma((PARTS + 1,)),
            ],
            compiler_params=pltpu.CompilerParams(vmem_limit_bytes=67043328),
        )(outs[0], outs[1])

    return jax.shard_map(local_step, mesh=mesh, in_specs=(act_spec, wgt_spec, act_spec),
                         out_specs=(act_spec, act_spec), check_vma=False)
```

time: 412 us -> 196 us (0.48)
  waiting for transfers between devices: 329 us -> 0 us
  Pallas kernels: 0 us -> 195 us
  matrix products: 65.4 us -> 0 us
  between operations: 13.8 us -> 0.8 us
    reduce_scatter x2 -> x0, waiting for transfers between devices: 269 us -> none  [the longest x1 222 us: local_step(): lax.psum_scatter(dw_part, ('data', 'row'), scatter_dimension=0, tiled=True)]
    pallas_call x0 -> x2, Pallas kernels: none -> 195 us  [the longest x1 189 us: local_step(): pl.pallas_call(functools.partial(kernel, nd, nc), out_shape=(jax.ShapeDty...]
    dot_general x2 -> x0, matrix products: 65.4 us -> none  [the longest x1 33.6 us: local_step(): lax.dot_general(x_rows, dy_blk, (((0,), (0,)), ((), ())), preferred_eleme...]
    all_gather x2 -> x0, waiting for transfers between devices: 58.8 us -> none  [the longest x1 42.8 us: local_step(): w_cols = lax.all_gather(w_blk, 'row', axis=0, tiled=True)]
  transfers between devices with their start and end apart: 4 -> 0, of which waited for: 4 -> 0; matrix products, arithmetic and copies ran while one was open for 17% -> 0% of each run, Pallas kernels for 0% -> 0%
where the time goes in v3:
time: 196 us
  Pallas kernels  195 us (99%)
    pallas_call x1, Pallas kernels, local_step(): pl.pallas_call(functools.partial(kernel, nd, nc), out_shape=(jax.ShapeDty...  189 us
    pallas_call x1, Pallas kernels, local_step(): pl.pallas_call(finish, out_shape=(jax.ShapeDtypeStruct((tokens, feats), B...  5.81 us

profile of v3, /device:TPU:97, one launch (start us, length us, event | category | flops | bytes accessed | tf_op | source)
XLA Modules:
  0.0 196.1 jit_solution(5275970560119856246)
XLA Ops:
  0.6 189.5 %shard_map.50 = (bf16[1024,512]{1,0:T(8,128)(2,1)}, f32[256,5504]{1,0:T(8,128)}, bf16[1024,5504]{1,0:T(8,128)(2,1)}, bf16[1024,5504]{1,0:T(8,128)(2,1)}, bf16[2,2048,1408]{2,1,0:T(8,128)(2,1)}) custom-call(bf16[1024,512]{1,0:T(8,128)(2,1)} %x_ref.1, bf16[1024,5504]{1,0:T(8,128)(2,1)} %w_ref.1, bf16[1024,5504]{1,0:T(8,128)(2,1)} %dy_ref.1), custom_call_target="tpu_custom_call" | custom-call | tf_op jit(solution)/shard_map/pallas_call | solution.py:438
  190.1 5.8 %shard_map.51 = (bf16[1024,512]{1,0:T(8,128)(2,1)}, f32[256,5504]{1,0:T(8,128)}) custom-call(bf16[1024,512]{1,0:T(8,128)(2,1)} %get-tuple-element.4.dx_in, f32[256,5504]{1,0:T(8,128)} %get-tuple-element.5.dw_in), custom_call_target="tpu_custom_call" | custom-call | tf_op jit(solution)/shard_map/pallas_call | solution.py:469

commit v4 on v3

--- a/solution.py
+++ b/solution.py
@@ -45,6 +45,9 @@
     def near(k):
         return (k + c - d + nd) % nd
 
+    def used(row, k):
+        return near(k) != (1 if row == 1 else 3)
+
     def start_of(e):
         k = (d + e) % nd
         return k * span - k // (nd - 1) * (nd * span - cols)
@@ -130,7 +133,10 @@
 
     for core in range(2):
         for up in range(2):
-            x_rows(up, core).start()
+            @pl.when(near(0) != 0)
+            def _(up=up, core=core):
+                x_rows(up, core).start()
+
             x_side(up, core).start()
     x_partner().start()
     w_swap(0).start()
@@ -201,10 +207,12 @@
     for up in range(2):
         x_pass(0, up).start()
     for row in (1, 2):
-        for who in range(2):
-            x_arrived(row, 0, who).wait_recv()
-        for up in range(2):
-            x_next(row, up).start()
+        @pl.when(used(row, 0))
+        def _(row=row):
+            for who in range(2):
+                x_arrived(row, 0, who).wait_recv()
+            for up in range(2):
+                x_next(row, up).start()
     w_swap(1).wait_recv()
     dx_run(soon, steps, 0)
     for copy in dx_loads(0, steps * DEPTH, rest):
@@ -250,8 +258,15 @@
         return (lcopy(dy_ref.at[:, cut(e, j)], buf.at[slot, mine, to], loc_d.at[slot, 0]),
                 lcopy(dyo.at[:, cut(e, j)], buf.at[slot, theirs, to], loc_d.at[slot, 1]))
 
+    def pass_on(row):
+        for up in range(2):
+            @pl.when(used(row, 3 if up else 1))
+            def _(up=up):
+                x_next(row, up).wait_recv()
+                x_pass(row, up).start()
+
     dy_swap().wait_recv()
-    work = [(e, j) for j in range(n) for e in (3, 2)] + [(e, j) for j in range(n) for e in (0, 1)]
+    work = [(e, j) for j in range(n) for e in (3, 2)]
     for copy in own_load(*work[0], 0):
         copy.start()
     x_arrived(0, 0, other).wait_recv()
@@ -263,18 +278,13 @@
                 copy.start()
         for copy in own_load(e, j, i % 2):
             copy.wait()
-        if e > 1:
-            heavy(3 - e, j, i % 2)
-        else:
-            light(e, j, i % 2)
+        heavy(3 - e, j, i % 2)
         if i == n:
-            for up in range(2):
-                x_next(1, up).wait_recv()
-                x_pass(1, up).start()
-        if i >= 2 * n and i % 2 and i // 2 - n < n - 1:
+            pass_on(1)
+        if i % 2 and i // 2 < n - 1:
             for side in range(2):
-                dy_give(side, i // 2 - n).wait_recv()
-                dy_share(side, i // 2 - n, mine).start()
+                dy_give(side, i // 2).wait_recv()
+                dy_share(side, i // 2, mine).start()
 
     def nbr_load(side, j, slot):
         to = pl.ds(0, subs[j][1])
@@ -297,7 +307,6 @@
                     y_msg(m, j).start()
 
     work = [(side, j) for j in range(n) for side in (1, 0)]
-    work = [(*item, (0, 3, 1)) for item in work] + [(*item, (2,)) for item in work]
     shared = set()
 
     def ready(side, j):
@@ -308,24 +317,42 @@
                 dy_share(side, j, mine).start()
             dy_share(side, j, theirs).wait_recv()
 
-    ready(*work[0][:2])
-    nbr_load(*work[0][:2], 0).start()
-    for i, (side, j, ks) in enumerate(work):
-        if i + 1 < len(work):
-            ready(*work[i + 1][:2])
-            nbr_load(*work[i + 1][:2], (i + 1) % 2).start()
-        nbr_load(side, j, i % 2).wait()
-        if i == 1:
-            for up in range(2):
-                x_next(2, up).wait_recv()
-                x_pass(2, up).start()
-            for m in range(4):
-                x_msg(m).start()
-        if i == 2 * n:
-            for row in (1, 2):
-                for who in range(2):
-                    x_arrived(row, 2, who).wait_recv()
-        add(side, j, i % 2, ks)
+    def add_all(ks, between):
+        ready(*work[0])
+        nbr_load(*work[0], 0).start()
+        for i, (side, j) in enumerate(work):
+            if i + 1 < len(work):
+                ready(*work[i + 1])
+                nbr_load(*work[i + 1], (i + 1) % 2).start()
+            nbr_load(side, j, i % 2).wait()
+            if i == 1:
+                between()
+            add(side, j, i % 2, ks)
+
+    def between():
+        pass_on(2)
+        for m in range(4):
+            x_msg(m).start()
+
+    add_all((0, 3, 1), between)
+
+    last = [(e, j) for j in range(n) for e in (0, 1)]
+    for copy in own_load(*last[0], 0):
+        copy.start()
+    for i, (e, j) in enumerate(last):
+        if i + 1 < len(last):
+            for copy in own_load(*last[i + 1], (i + 1) % 2):
+                copy.start()
+        for copy in own_load(e, j, i % 2):
+            copy.wait()
+        light(e, j, i % 2)
+
+    for row in (1, 2):
+        @pl.when(used(row, 2))
+        def _(row=row):
+            for who in range(2):
+                x_arrived(row, 2, who).wait_recv()
+    add_all((2,), lambda: None)
 
     def pass_y(j):
         at = pl.ds(*subs[j])
@@ -357,10 +384,8 @@
             for e in pair:
                 y_msg((5, 4, 2, 3)[e], j).wait_recv()
                 mine_of(e)[:, at] += tail_y[(2, 3, 1, 0)[e], :, at]
-            if j:
-                for e in pair:
+                if j:
                     out_y(e, j - 1).wait()
-            for e in pair:
                 out_y(e, j).start()
         for e in pair:
             out_y(e, n - 1).wait()
@@ -372,17 +397,23 @@
         rows = pl.ds(t * deep, deep)
         buf[1, rows, 0:quarter] = (acc[0, t] + tail_x[t, 0] + tail_x[t, 1]).astype(BF16)
         lcopy(buf.at[1, rows, pl.ds(0, quarter)], dx_ref.at[rows], loc_dx.at[t]).start()
-    done_y((0, 1))
-
     x_partner().wait_send()
     for up in range(2):
         for core in range(2):
             x_side(up, core).wait_send()
-            x_rows(up, core).wait_send()
-        for row in range(3):
-            x_pass(row, up).wait_send()
+
+            @pl.when(near(0) != 0)
+            def _(up=up, core=core):
+                x_rows(up, core).wait_send()
+        x_pass(0, up).wait_send()
         for row in (1, 2):
-            x_next(row, up).wait_send()
+            @pl.when(used(row, 3 if up else 1))
+            def _(row=row, up=up):
+                x_pass(row, up).wait_send()
+
+            @pl.when(used(row, 0))
+            def _(row=row, up=up):
+                x_next(row, up).wait_send()
     for t in range(2):
         rows = pl.ds(t * deep, deep)
         lcopy(buf.at[1, rows, pl.ds(0, quarter)], dx_ref.at[rows], loc_dx.at[t]).wait()
@@ -394,7 +425,11 @@
         for side in range(2):
             dy_give(side, j).wait_send()
             dy_share(side, j, mine).wait_send()
-        for m in range(6):
+        for m in range(4):
+            y_msg(m, j).wait_send()
+    done_y((0, 1))
+    for j in range(n):
+        for m in (4, 5):
             y_msg(m, j).wait_send()
 
 

time: 196 us -> 196 us (level)
  no operation moved by 1% of the time
where the time goes in v4:
time: 196 us
  Pallas kernels  195 us (99%)
    pallas_call x1, Pallas kernels, local_step(): pl.pallas_call(functools.partial(kernel, nd, nc), out_shape=(jax.ShapeDty...  189 us
    pallas_call x1, Pallas kernels, local_step(): pl.pallas_call(finish, out_shape=(jax.ShapeDtypeStruct((tokens, feats), B...  5.81 us

profile of v4, /device:TPU:97, one launch (start us, length us, event | category | flops | bytes accessed | tf_op | source)
XLA Modules:
  0.0 195.6 jit_solution(13952805192589861943)
XLA Ops:
  0.6 188.9 %shard_map.50 = (bf16[1024,512]{1,0:T(8,128)(2,1)}, f32[256,5504]{1,0:T(8,128)}, bf16[1024,5504]{1,0:T(8,128)(2,1)}, bf16[1024,5504]{1,0:T(8,128)(2,1)}, bf16[2,2048,1408]{2,1,0:T(8,128)(2,1)}) custom-call(bf16[1024,512]{1,0:T(8,128)(2,1)} %x_ref.1, bf16[1024,5504]{1,0:T(8,128)(2,1)} %w_ref.1, bf16[1024,5504]{1,0:T(8,128)(2,1)} %dy_ref.1), custom_call_target="tpu_custom_call" | custom-call | tf_op jit(solution)/shard_map/pallas_call | solution.py:473
  189.6 5.8 %shard_map.51 = (bf16[1024,512]{1,0:T(8,128)(2,1)}, f32[256,5504]{1,0:T(8,128)}) custom-call(bf16[1024,512]{1,0:T(8,128)(2,1)} %get-tuple-element.4.dx_in, f32[256,5504]{1,0:T(8,128)} %get-tuple-element.5.dw_in), custom_call_target="tpu_custom_call" | custom-call | tf_op jit(solution)/shard_map/pallas_call | solution.py:504

commit v5 on v4

--- a/solution.py
+++ b/solution.py
@@ -89,7 +89,7 @@
     def dy_swap():
         return rcopy(dy_ref, dyo, sem_a, rem_a, row=other)
 
-    soon = cols // DEPTH * 2 // 5
+    soon = cols // DEPTH * 3 // 10
     halves = ((0, soon * DEPTH), (soon * DEPTH, cols - soon * DEPTH))
 
     def w_swap(i):
@@ -265,27 +265,6 @@
                 x_next(row, up).wait_recv()
                 x_pass(row, up).start()
 
-    dy_swap().wait_recv()
-    work = [(e, j) for j in range(n) for e in (3, 2)]
-    for copy in own_load(*work[0], 0):
-        copy.start()
-    x_arrived(0, 0, other).wait_recv()
-    for who in range(2):
-        x_arrived(0, 2, who).wait_recv()
-    for i, (e, j) in enumerate(work):
-        if i + 1 < len(work):
-            for copy in own_load(*work[i + 1], (i + 1) % 2):
-                copy.start()
-        for copy in own_load(e, j, i % 2):
-            copy.wait()
-        heavy(3 - e, j, i % 2)
-        if i == n:
-            pass_on(1)
-        if i % 2 and i // 2 < n - 1:
-            for side in range(2):
-                dy_give(side, i // 2).wait_recv()
-                dy_share(side, i // 2, mine).start()
-
     def nbr_load(side, j, slot):
         to = pl.ds(0, subs[j][1])
         return lcopy(nbr.at[side, :, pl.ds(*subs[j])], buf.at[slot, :, to], loc_n.at[slot])
@@ -306,7 +285,6 @@
                 def _(m=m):
                     y_msg(m, j).start()
 
-    work = [(side, j) for j in range(n) for side in (1, 0)]
     shared = set()
 
     def ready(side, j):
@@ -317,24 +295,64 @@
                 dy_share(side, j, mine).start()
             dy_share(side, j, theirs).wait_recv()
 
-    def add_all(ks, between):
-        ready(*work[0])
-        nbr_load(*work[0], 0).start()
-        for i, (side, j) in enumerate(work):
+    def heavies(j):
+        return [(True, e, j) for e in (3, 2)]
+
+    def adds(j):
+        return [(False, side, j) for side in (1, 0)]
+
+    def run(work, ks, before):
+        def load(i):
+            own_tokens, e, j = work[i]
+            if own_tokens:
+                return own_load(e, j, i % 2)
+            ready(e, j)
+            return (nbr_load(e, j, i % 2),)
+
+        def wait(i):
+            own_tokens, e, j = work[i]
+            for copy in own_load(e, j, i % 2) if own_tokens else (nbr_load(e, j, i % 2),):
+                copy.wait()
+
+        for copy in load(0):
+            copy.start()
+        for i, (own_tokens, e, j) in enumerate(work):
+            before(i)
             if i + 1 < len(work):
-                ready(*work[i + 1])
-                nbr_load(*work[i + 1], (i + 1) % 2).start()
-            nbr_load(side, j, i % 2).wait()
-            if i == 1:
-                between()
-            add(side, j, i % 2, ks)
-
-    def between():
-        pass_on(2)
-        for m in range(4):
-            x_msg(m).start()
-
-    add_all((0, 3, 1), between)
+                for copy in load(i + 1):
+                    copy.start()
+            wait(i)
+            if own_tokens:
+                heavy(3 - e, j, i % 2)
+            else:
+                add(e, j, i % 2, ks)
+
+    work = [item for j in range(n - 1) for item in heavies(j)] + adds(0) + heavies(n - 1)
+    first = 2 * n - 2
+    work += [item for j in range(1, n) for item in adds(j)]
+
+    def share(j):
+        for side in range(2):
+            dy_give(side, j).wait_recv()
+            dy_share(side, j, mine).start()
+
+    def before(i):
+        if i == first - 1:
+            share(0)
+            pass_on(1)
+        if i == first + 1:
+            pass_on(2)
+            for m in range(4):
+                x_msg(m).start()
+        if i == first + 2:
+            for j in range(1, n - 1):
+                share(j)
+
+    dy_swap().wait_recv()
+    x_arrived(0, 0, other).wait_recv()
+    for who in range(2):
+        x_arrived(0, 2, who).wait_recv()
+    run(work, (0, 3, 1), before)
 
     last = [(e, j) for j in range(n) for e in (0, 1)]
     for copy in own_load(*last[0], 0):
@@ -352,7 +370,7 @@
         def _(row=row):
             for who in range(2):
                 x_arrived(row, 2, who).wait_recv()
-    add_all((2,), lambda: None)
+    run([item for j in range(n) for item in adds(j)], (2,), lambda i: None)
 
     def pass_y(j):
         at = pl.ds(*subs[j])

time: 196 us -> 196 us (level)
  no operation moved by 1% of the time
where the time goes in v5:
time: 196 us; the launch traced here: 195 us
  Pallas kernels  195 us (99%)
    pallas_call x1, Pallas kernels, local_step(): pl.pallas_call(functools.partial(kernel, nd, nc), out_shape=(jax.ShapeDty...  189 us
    pallas_call x1, Pallas kernels, local_step(): pl.pallas_call(finish, out_shape=(jax.ShapeDtypeStruct((tokens, feats), B...  5.81 us

profile of v5, /device:TPU:97, one launch (start us, length us, event | category | flops | bytes accessed | tf_op | source)
XLA Modules:
  0.0 195.4 jit_solution(9986311377623768476)
XLA Ops:
  0.6 188.8 %shard_map.50 = (bf16[1024,512]{1,0:T(8,128)(2,1)}, f32[256,5504]{1,0:T(8,128)}, bf16[1024,5504]{1,0:T(8,128)(2,1)}, bf16[1024,5504]{1,0:T(8,128)(2,1)}, bf16[2,2048,1408]{2,1,0:T(8,128)(2,1)}) custom-call(bf16[1024,512]{1,0:T(8,128)(2,1)} %x_ref.1, bf16[1024,5504]{1,0:T(8,128)(2,1)} %w_ref.1, bf16[1024,5504]{1,0:T(8,128)(2,1)} %dy_ref.1), custom_call_target="tpu_custom_call" | custom-call | tf_op jit(solution)/shard_map/pallas_call | solution.py:491
  189.4 5.8 %shard_map.51 = (bf16[1024,512]{1,0:T(8,128)(2,1)}, f32[256,5504]{1,0:T(8,128)}) custom-call(bf16[1024,512]{1,0:T(8,128)(2,1)} %get-tuple-element.4.dx_in, f32[256,5504]{1,0:T(8,128)} %get-tuple-element.5.dw_in), custom_call_target="tpu_custom_call" | custom-call | tf_op jit(solution)/shard_map/pallas_call | solution.py:522
